TPU v7x, 8 devices: a whole 2x2x1 slice. The times are simulated.
8 devices in a mesh: dp: 2 (over z, y), sp: 4 (over x, core).
Axes of the slice: x: 2, y: 2, z: 1, core: 2. Of those that a mesh axis runs over, the one named last changes fastest.
Arguments:
- x_patch: bfloat16 [64, 4096, 1024], P('dp', 'sp'), parts along dimension 0
- w_tok1: bfloat16 [4096, 512], P('sp')
- b_tok1: float32 [512], P('sp')
- w_tok2: bfloat16 [512, 4096], P(None, 'sp')
- b_tok2: float32 [4096], P('sp')
- w_ch1: bfloat16 [1024, 4096], replicated
- b_ch1: float32 [4096], replicated
- w_ch2: bfloat16 [4096, 1024], replicated
- b_ch2: float32 [1024], replicated
- ln1_gain: float32 [1024], replicated
- ln1_bias: float32 [1024], replicated
- ln2_gain: float32 [1024], replicated
- ln2_bias: float32 [1024], replicated
Outputs:
- output: bfloat16 [64, 4096, 1024], P('dp', 'sp'), parts along dimension 0
There are 2 independent parts. A program takes and returns all parts, laid end to end along the dimension named above; an argument that names none is the same for every part.
All inputs are finite; a program needn't handle non-finite values.
Results may differ from a plain program's by a relative error of at most 0.00987915.
Values are sent between devices in bfloat16 or wider.
A program may use at most 1 GiB of HBM per device.

v0:
```python
import jax
import jax.numpy as jnp
from jax import lax
from jax.sharding import PartitionSpec as P

LN_EPS = 1e-6


def layer_norm(values, ln_gain, ln_bias):
    mean_val = jnp.mean(values, axis=-1, keepdims=True)
    centred = values - mean_val
    var_val = jnp.mean(centred * centred, axis=-1, keepdims=True)
    return centred * lax.rsqrt(var_val + LN_EPS) * ln_gain + ln_bias


def channel_mix(x_mid, w_ch1, b_ch1, w_ch2, b_ch2, ln2_gain, ln2_bias):
    mid_wide = x_mid.astype(jnp.float32)
    normed_two = layer_norm(mid_wide, ln2_gain, ln2_bias).astype(jnp.bfloat16)
    ch_pre = jnp.einsum("bsc,cf->bsf", normed_two, w_ch1, preferred_element_type=jnp.float32) + b_ch1
    ch_act = jax.nn.gelu(ch_pre).astype(jnp.bfloat16)
    ch_out = jnp.einsum("bsf,fc->bsc", ch_act, w_ch2, preferred_element_type=jnp.float32) + b_ch2
    return (mid_wide + ch_out).astype(jnp.bfloat16)


def solution(mesh):
    row_spec = P("dp", "sp", None)

    def local_layer(x_blk, w1_rows, b1_part, w2_cols, b2_part, w_ch1, b_ch1, w_ch2, b_ch2, ln1_gain, ln1_bias, ln2_gain, ln2_bias):
        x_wide = x_blk.astype(jnp.float32)
        normed = layer_norm(x_wide, ln1_gain, ln1_bias).astype(jnp.bfloat16)
        part_pre = jnp.einsum("bsc,sd->bdc", normed, w1_rows, preferred_element_type=jnp.float32)
        tok_pre = lax.psum_scatter(part_pre, "sp", scatter_dimension=1, tiled=True) + b1_part[None, :, None]
        tok_act = jax.nn.gelu(tok_pre).astype(jnp.bfloat16)
        act_full = lax.all_gather(tok_act, "sp", axis=1, tiled=True)
        tok_out = jnp.einsum("bdc,ds->bsc", act_full, w2_cols, preferred_element_type=jnp.float32) + b2_part[None, :, None]
        x_mid = (x_wide + tok_out).astype(jnp.bfloat16)
        return channel_mix(x_mid, w_ch1, b_ch1, w_ch2, b_ch2, ln2_gain, ln2_bias)

    in_specs = (row_spec, P("sp", None), P("sp"), P(None, "sp"), P("sp"), P(None, None), P(None), P(None, None), P(None), P(None), P(None), P(None), P(None))
    return jax.shard_map(local_layer, mesh=mesh, in_specs=in_specs, out_specs=row_spec, check_vma=False)
```

profile of v0, /device:TPU:0, one launch (start us, length us, event | category | flops | bytes accessed | tf_op | source)
XLA Modules:
  0.0 1792.3 jit_solution(17055950763743312130)
XLA Ops:
  6.5 0.0 copy-start
  6.5 0.0 reduce-scatter.2.cloned.1.call-start
  6.6 87.5 %copy.14 = bf16[32,1024,1024]{1,2,0:T(8,128)(2,1)} copy(bf16[32,1024,1024]{2,1,0:T(8,128)(2,1)} %param.13) | data formatting | bytes 134217728 | tf_op args[0]
  94.1 20.8 %convert_reduce_fusion.1 = f32[32,1024]{1,0:T(8,128)S(1)} fusion(bf16[32,1024,1024]{1,2,0:T(8,128)(2,1)} %copy.14), kind=kLoop, calls=%fused_computation.16 | loop fusion | flops 67076096 | bytes 67239936 | tf_op jit(solution)/shard_map/reduce_sum | solution.py:10
  114.9 21.5 %fusion.20 = f32[32,1024]{1,0:T(8,128)S(1)} fusion(bf16[32,1024,1024]{1,2,0:T(8,128)(2,1)} %copy.14, f32[32,1024]{1,0:T(8,128)S(1)} %broadcast_multiply_fusion.1), kind=kLoop, calls=%fused_computation.25 | loop fusion | flops 134184960 | bytes 67371008 | tf_op jit(solution)/shard_map/reduce_sum | solution.py:12
  136.4 0.0 copy-done.5
  136.4 0.0 copy-done.6
  136.4 0.0 copy-done.3
  136.4 0.0 copy-start.2
  136.4 0.0 copy-start.7
  136.5 54.2 %fusion.46 = f32[32,512,1024]{1,2,0:T(8,128)} fusion(bf16[32,1024,1024]{1,2,0:T(8,128)(2,1)} %copy.14, f32[1024]{0:T(1024)S(1)} %copy-done.5, f32[1024]{0:T(1024)S(1)} %copy-done.6, f32[32,1024]{1,0:T(8,128)S(1)} %add_rsqrt_fusion.1, f32[32,1024]{1,0:T(8,128)S(1)} %broadcast_multiply_fusion.1, bf16[1024,512]{1,0:T(8,128)(2,1)S(1)} %copy-done.3), kind=kOutput, calls=%fused_computation.40 | convolution fusion | flops 34561064960 | bytes 135536640 | tf_op jit(solution)/shard_map/bsc,sd->bdc/dot_general | solution.py:31
  190.7 0.0 reduce-scatter.2.cloned.1.call-update
  190.7 0.2 all-gather.2.cloned.1.call-start
  190.9 443.3 %reduce-scatter.2.cloned.1.call-done = f32[32,128,1024]{1,2,0:T(8,128)} async-done(((f32[32,512,1024]{1,2,0:T(8,128)}), f32[32,128,1024]{1,2,0:T(8,128)}) %reduce-scatter.2.cloned.1.call-update) | async-done | bytes 16777232 | tf_op jit(solution)/shard_map/reduce_scatter | solution.py:32
  634.2 0.0 copy-done.2
  634.2 11.7 fusion.56
  645.9 0.0 all-gather.2.cloned.1.call-update
  646.0 0.0 copy-start.4
  646.0 0.0 copy-start.8
  646.0 0.0 copy-start.9
  646.0 204.0 %all-gather.2.cloned.1.call-done = bf16[32,512,1024]{1,2,0:T(8,128)(2,1)} async-done(((bf16[32,128,1024]{1,2,0:T(8,128)(2,1)}), bf16[32,512,1024]{1,2,0:T(8,128)(2,1)}) %all-gather.2.cloned.1.call-update) | async-done | bytes 33554448 | tf_op jit(solution)/shard_map/all_gather | solution.py:34
  850.0 0.0 copy-done
  850.0 0.0 copy-done.7
  850.0 66.4 %convert_reduce_fusion = (f32[32,1024]{1,0:T(8,128)S(1)}, bf16[32,1024,1024]{1,2,0:T(8,128)(2,1)}) fusion(f32[1024]{0:T(1024)S(1)} %copy-done.7, bf16[32,512,1024]{1,2,0:T(8,128)(2,1)} %all-gather.2.cloned.1.call-done, bf16[512,1024]{1,0:T(8,128)(2,1)S(1)} %copy-done, bf16[32,1024,1024]{1,2,0:T(8,128)(2,1)} %copy.14), kind=kOutput, calls=%fused_computation.13 | convolution fusion | flops 34561032192 | bytes 168955904 | tf_op jit(solution)/shard_map/bdc,ds->bsc/dot_general | solution.py:35
  916.4 21.5 %fusion.16 = f32[32,1024]{1,0:T(8,128)S(1)} fusion(bf16[32,1024,1024]{1,2,0:T(8,128)(2,1)} %get-tuple-element.6, f32[32,1024]{1,0:T(8,128)S(1)} %broadcast_multiply_fusion), kind=kLoop, calls=%fused_computation.21 | loop fusion | flops 134184960 | bytes 67371008 | tf_op jit(solution)/shard_map/reduce_sum | solution.py:12
  937.9 0.0 copy-done.4
  937.9 0.0 copy-done.8
  937.9 0.0 copy-start.10
  938.0 439.2 %fusion.76 = bf16[32,1024,4096]{2,1,0:T(8,128)(2,1)} fusion(f32[4096]{0:T(1024)S(1)} %copy-done.4, bf16[32,1024,1024]{1,2,0:T(8,128)(2,1)} %get-tuple-element.6, f32[1024]{0:T(1024)S(1)} %copy-done.8, f32[1024]{0:T(1024)S(1)} %copy-done.9, f32[32,1024]{1,0:T(8,128)S(1)} %add_rsqrt_fusion, ...), kind=kOutput, calls=%fused_computation.8.clone.clone.clone.clone.1 | convolution fusion | flops 276421410816 | bytes 344219648 | tf_op jit(solution)/shard_map/bsc,cf->bsf/dot_general | solution.py:19
  1377.2 0.0 copy-start.1
  1377.2 320.5 %fusion.25 = bf16[32,1024,1024]{1,2,0:T(8,128)(2,1)} fusion(bf16[32,1024,1024]{1,2,0:T(8,128)(2,1)} %get-tuple-element.6, f32[1024]{0:T(1024)S(1)} %copy-done.10, bf16[4096,1024]{1,0:T(8,128)(2,1)} %param.20, bf16[32,1024,4096]{2,1,0:T(8,128)(2,1)} %fusion.76), kind=kOutput, calls=%fused_computation.30 | convolution fusion | flops 275012124672 | bytes 411045888 | tf_op jit(solution)/shard_map/bsf,fc->bsc/dot_general | solution.py:21
  1697.7 87.3 %copy.17 = bf16[32,1024,1024]{2,1,0:T(8,128)(2,1)} copy(bf16[32,1024,1024]{1,2,0:T(8,128)(2,1)} %fusion.25) | data formatting | bytes 134217728 | tf_op jit(solution)/shard_map/convert_element_type | solution.py:22
  (10 shorter events, 0.1 us)
Async XLA Ops:
  6.5 843.4 %copy-start = (bf16[512,1024]{1,0:T(8,128)(2,1)S(1)}, bf16[512,1024]{1,0:T(8,128)(2,1)}, u32[]{:S(2)}) copy-start(bf16[512,1024]{1,0:T(8,128)(2,1)} %param.16) | copy-start | bytes 3145732
  6.5 129.9 %copy-start.5 = (f32[1024]{0:T(1024)S(1)}, f32[1024]{0:T(1024)}, u32[]{:S(2)}) copy-start(f32[1024]{0:T(1024)} %param.23) | copy-start | bytes 12292
  6.5 129.9 %copy-start.6 = (f32[1024]{0:T(1024)S(1)}, f32[1024]{0:T(1024)}, u32[]{:S(2)}) copy-start(f32[1024]{0:T(1024)} %param.22) | copy-start | bytes 12292
  6.5 129.9 %copy-start.3 = (bf16[1024,512]{1,0:T(8,128)(2,1)S(1)}, bf16[1024,512]{1,0:T(8,128)(2,1)}, u32[]{:S(2)}) copy-start(bf16[1024,512]{1,0:T(8,128)(2,1)} %param.14) | copy-start | bytes 3145732
  6.5 627.7 %reduce-scatter.2.cloned.1.call-start = ((), (), s32[]{:S(2)}) async-start(), calls=%async_computation.1 | async-start | bytes 83886080 | tf_op jit(solution)/shard_map/reduce_scatter | solution.py:32
  136.4 497.8 %copy-start.2 = (f32[128]{0:T(128)S(1)}, f32[128]{0:T(128)}, u32[]{:S(2)}) copy-start(f32[128]{0:T(128)} %param.15) | copy-start | bytes 1540
  136.4 713.5 %copy-start.7 = (f32[1024]{0:T(1024)S(1)}, f32[1024]{0:T(1024)}, u32[]{:S(2)}) copy-start(f32[1024]{0:T(1024)} %param.17) | copy-start | bytes 12292
  190.7 659.3 %all-gather.2.cloned.1.call-start = ((), (), s32[]{:S(2)}) async-start(), calls=%async_computation.2 | async-start | bytes 41943040 | tf_op jit(solution)/shard_map/all_gather | solution.py:34
  646.0 291.9 %copy-start.4 = (f32[4096]{0:T(1024)S(1)}, f32[4096]{0:T(1024)}, u32[]{:S(2)}) copy-start(f32[4096]{0:T(1024)} %param.19) | copy-start | bytes 49156
  646.0 291.9 %copy-start.8 = (f32[1024]{0:T(1024)S(1)}, f32[1024]{0:T(1024)}, u32[]{:S(2)}) copy-start(f32[1024]{0:T(1024)} %param.25) | copy-start | bytes 12292
  646.0 291.9 %copy-start.9 = (f32[1024]{0:T(1024)S(1)}, f32[1024]{0:T(1024)}, u32[]{:S(2)}) copy-start(f32[1024]{0:T(1024)} %param.24) | copy-start | bytes 12292
  937.9 439.2 %copy-start.10 = (f32[1024]{0:T(1024)S(1)}, f32[1024]{0:T(1024)}, u32[]{:S(2)}) copy-start(f32[1024]{0:T(1024)} %param.21) | copy-start | bytes 12292
  1377.2 407.8 %copy-start.1 = (bf16[512,1024]{1,0:T(8,128)(2,1)S(1)}, bf16[512,1024]{1,0:T(8,128)(2,1)}, u32[]{:S(2)}) copy-start(bf16[512,1024]{1,0:T(8,128)(2,1)} %param.16) | copy-start | bytes 3145732
Sparse Core Ops, SparseCore 0:
  190.8 443.3 reduce-scatter.1
  646.1 203.8 all-gather.1
where the time goes:
time: 1800 us; the launch traced here: 1790 us
  matrix products  880 us (49%)
  waiting for transfers between devices  647 us (36%)
  local copies, waits for them, and re-layouts  175 us (10%)
  other arithmetic  75.6 us (4%)
    reduce_scatter x1, waiting for transfers between devices, local_layer(): lax.psum_scatter(part_pre, 'sp', scatter_dimension=1, tiled=True)  443 us
    dot_general x1, matrix products, channel_mix(): jnp.einsum('bsc,cf->bsf', normed_two, w_ch1, preferred_element_type=jnp.f...  439 us
    dot_general x1, matrix products, channel_mix(): jnp.einsum('bsf,fc->bsc', ch_act, w_ch2, preferred_element_type=jnp.float32)  320 us
    all_gather x1, waiting for transfers between devices, local_layer(): act_full = lax.all_gather(tok_act, 'sp', axis=1, tiled=True)  204 us
    unnamed x23, local copies, waits for them, and re-layouts  87.5 us
    convert_element_type x1, local copies, waits for them, and re-layouts, channel_mix(): return (mid_wide + ch_out).astype(jnp.bfloat16)  87.3 us
    dot_general x1, matrix products, local_layer(): jnp.einsum('bdc,ds->bsc', act_full, w2_cols, preferred_element_type=jnp.f...  66.4 us
    dot_general x1, matrix products, local_layer(): jnp.einsum('bsc,sd->bdc', normed, w1_rows, preferred_element_type=jnp.flo...  54.2 us
  transfers between devices with their start and end apart: 2, of which 2 were waited for; matrix products, arithmetic and copies ran while one was open for 0% of the time, Pallas kernels for 0%

commit v1 on v0

v1 whole, which is shorter than its diff:
```python
import functools

import jax
import jax.numpy as jnp
from jax import lax
from jax.experimental import pallas as pl
from jax.experimental.pallas import tpu as pltpu
from jax.sharding import PartitionSpec as P

LN_EPS = 1e-6
GELU_C0 = 0.7978845608028654
GELU_C1 = GELU_C0 * 0.044715
HID_STEP = 512
ROW_HALF = 512
BLOCK = 256
SMALL = 32
TAIL = 2
LAG = 3
F32 = jnp.float32
BF16 = jnp.bfloat16
MESH_ID = pl.DeviceIdType.MESH


def gelu(a):
    half = 0.5 * a
    return half + half * jnp.tanh(a * (GELU_C0 + GELU_C1 * (a * a)))


def norm_rows(wide, gain, bias):
    mean = jnp.mean(wide, axis=-1, keepdims=True)
    centred = wide - mean
    var = jnp.mean(centred * centred, axis=-1, keepdims=True)
    return centred * lax.rsqrt(var + LN_EPS) * gain + bias


def token_in(x_ref, w1t_ref, gain_ref, bias_ref, part_ref, u_ref):
    rows = x_ref.shape[1]
    for k in range(0, rows, BLOCK):
        for r in range(k, k + BLOCK, SMALL):
            wide = x_ref[0, r : r + SMALL, :].astype(F32)
            u_ref[r : r + SMALL, :] = norm_rows(wide, gain_ref[...], bias_ref[...]).astype(BF16)
        term = jnp.dot(w1t_ref[:, k : k + BLOCK], u_ref[k : k + BLOCK, :], preferred_element_type=F32)
        term = term.reshape(part_ref.shape)
        if k == 0:
            part_ref[...] = term
        else:
            part_ref[...] += term


def weight_copies(wc1_hbm, wc2_hbm, wc1_ref, wc2_ref, sems, j):
    cols = pl.ds(pl.multiple_of(j * HID_STEP, HID_STEP), HID_STEP)
    return (
        pltpu.make_async_copy(wc1_hbm.at[:, cols], wc1_ref.at[j], sems.at[0, j]),
        pltpu.make_async_copy(wc2_hbm.at[cols, :], wc2_ref.at[j], sems.at[1, j]),
    )


def channel_mix(x_ref, g, w2t_ref, b2_ref, gain_ref, bias_ref, bc1_ref, bc2_ref, wc1_ref, wc2_ref, work, put, arrive):
    acc_ref, v_ref, h_a, h_b, a_a, a_b = work
    rows = x_ref.shape[1]
    steps = wc1_ref.shape[0]
    for k in range(0, rows, BLOCK):
        acc_ref[k : k + BLOCK, :] = jnp.dot(w2t_ref[k : k + BLOCK, :], g, preferred_element_type=F32)
        for r in range(k, k + BLOCK, SMALL):
            cut = slice(r, r + SMALL)
            mid = (x_ref[0, cut, :].astype(F32) + (acc_ref[cut, :] + b2_ref[cut, :])).astype(BF16).astype(F32)
            acc_ref[cut, :] = mid
            v_ref[cut, :] = norm_rows(mid, gain_ref[...], bias_ref[...]).astype(BF16)

    top, low = slice(0, ROW_HALF), slice(ROW_HALF, 2 * ROW_HALF)

    def up(j, cut, h_ref):
        h_ref[...] = jnp.dot(v_ref[cut, :], wc1_ref[j], preferred_element_type=F32)

    def act(j, h_ref, a_ref):
        bias = bc1_ref[j]
        for r in range(0, ROW_HALF, SMALL):
            a_ref[r : r + SMALL, :] = gelu(h_ref[r : r + SMALL, :] + bias).astype(BF16)

    def down(j, cut, a_ref):
        acc_ref[cut, :] += jnp.dot(a_ref[...], wc2_ref[j], preferred_element_type=F32)

    arrive(0)
    up(0, top, h_a)

    @pl.loop(0, steps - 1)
    def _(j):
        up(j, low, h_b)
        act(j, h_a, a_a)
        down(j, top, a_a)
        arrive(j + 1)
        up(j + 1, top, h_a)
        act(j, h_b, a_b)
        down(j, low, a_b)

    up(steps - 1, low, h_b)
    act(steps - 1, h_a, a_a)
    down(steps - 1, top, a_a)
    act(steps - 1, h_b, a_b)
    down(steps - 1, low, a_b)
    for r in range(0, rows, SMALL):
        cut = slice(r, r + SMALL)
        put(cut, (acc_ref[cut, :] + bc2_ref[...]).astype(BF16))


def mixer_kernel(
    images,
    xa_ref, xb_ref, w1t_ref, b1_ref, w2t_ref, b2_ref, gain1_ref, bias1_ref, gain2_ref, bias2_ref, bc1_ref, bc2_ref,
    wc1_hbm, wc2_hbm,
    z_ref, tail_hbm,
    wc1_ref, wc2_ref, acc_ref, v_ref, h_a, h_b, a_a, a_b,
    part_ref, pair_ref, own_ref, out_ref, far_ref, full_ref,
    w_sems, pair_send, pair_recv, far_send, far_recv, near_send, near_recv, wide_send, wide_recv, fwd_send, fwd_recv, tail_sem,
):
    t = pl.program_id(0)
    rank = lax.axis_index("sp")
    core = lax.rem(rank, 2)
    chip = rank // 2
    partner = chip * 2 + (1 - core)
    across = (1 - chip) * 2 + core
    kept = images - TAIL
    steps = wc1_ref.shape[0]

    def to(peer, src, dst, send, recv):
        return pltpu.make_async_remote_copy(
            src_ref=src, dst_ref=dst, send_sem=send, recv_sem=recv, device_id={"sp": peer}, device_id_type=MESH_ID
        )

    def pair_copy(i):
        slot = lax.rem(i, 2)
        return to(partner, part_ref.at[:, 1 - core], pair_ref.at[slot], pair_send, pair_recv.at[slot])

    def far_copy(i):
        slot = lax.rem(i, 2)
        return to(across, out_ref, far_ref.at[slot], far_send, far_recv.at[slot])

    def near_copy(i):
        slot = lax.rem(i, 3)
        return to(partner, full_ref.at[slot, rank], full_ref.at[slot, rank], near_send, near_recv.at[slot])

    def wide_copy(i):
        slot = lax.rem(i, 3)
        return to(across, full_ref.at[slot, rank], full_ref.at[slot, rank], wide_send, wide_recv.at[slot])

    def fwd_copy(i):
        slot = lax.rem(i, 3)
        return to(partner, full_ref.at[slot, across], full_ref.at[slot, across], fwd_send, fwd_recv.at[slot])

    def tail_copy(i):
        return pltpu.make_async_copy(full_ref.at[lax.rem(i, 3)], tail_hbm.at[i - kept], tail_sem)

    @pl.when(t == 0)
    def _():
        barrier = pltpu.get_barrier_semaphore()
        for peer in (partner, across):
            pl.semaphore_signal(barrier, inc=1, device_id={"sp": peer}, device_id_type=MESH_ID)
        for j in range(steps):
            for copy in weight_copies(wc1_hbm, wc2_hbm, wc1_ref, wc2_ref, w_sems, j):
                copy.start()
        pl.semaphore_wait(barrier, 2)

    @pl.when(t >= 3)
    def _():
        i = t - 3
        wide_copy(i).wait_recv()
        fwd_copy(i).start()

    @pl.when(jnp.logical_and(t >= 2, t < images + 2))
    def _():
        i = t - 2
        far_copy(i).wait_recv()

        @pl.when(t >= 3)
        def _():
            near_copy(i).wait_send()
            wide_copy(i).wait_send()

        slot = lax.rem(i, 3)
        cut_rows = own_ref.shape[0]
        for r in range(0, cut_rows, SMALL):
            cut = slice(r, r + SMALL)
            total = (own_ref[cut, :] + far_ref[lax.rem(i, 2), cut, :]) + b1_ref[cut, :]
            full_ref[slot, rank, cut, :] = gelu(total).astype(BF16)

    @pl.when(jnp.logical_and(t >= 1, t < images + 1))
    def _():
        i = t - 1
        slot = lax.rem(i, 2)
        pair_copy(i).wait_recv()

        @pl.when(t >= 2)
        def _():
            far_copy(i).wait_send()

        own_ref[...] = part_ref[chip, core] + pair_ref[slot, chip]
        out_ref[...] = part_ref[1 - chip, core] + pair_ref[slot, 1 - chip]

    @pl.when(jnp.logical_and(t >= 1, t <= images))
    def _():
        pair_copy(t - 1).wait_send()

    @pl.when(jnp.logical_and(t >= 2, t < images + 2))
    def _():
        near_copy(t - 2).start()

    @pl.when(jnp.logical_and(t >= 1, t < images + 1))
    def _():
        far_copy(t - 1).start()

    @pl.when(jnp.logical_and(t >= 2, t < images + 2))
    def _():
        wide_copy(t - 2).start()

    @pl.when(t < images)
    def _():
        token_in(xa_ref, w1t_ref, gain1_ref, bias1_ref, part_ref, v_ref)
        pair_copy(t).start()

    @pl.when(t == 2)
    def _():
        for j in range(steps):
            for copy in weight_copies(wc1_hbm, wc2_hbm, wc1_ref, wc2_ref, w_sems, j):
                copy.wait()

    @pl.when(t >= 3)
    def _():
        i = t - 3
        near_copy(i).wait_recv()
        fwd_copy(i).wait_recv()

    @pl.when(jnp.logical_and(t >= 3, t < kept + 3))
    def _():
        g = full_ref[lax.rem(t, 3)].reshape(-1, full_ref.shape[3])

        def put(cut, value):
            z_ref[0, cut, :] = value

        channel_mix(
            xb_ref, g, w2t_ref, b2_ref, gain2_ref, bias2_ref, bc1_ref, bc2_ref, wc1_ref, wc2_ref,
            (acc_ref, v_ref, h_a, h_b, a_a, a_b), put, lambda j: None,
        )

    @pl.when(t >= kept + 3)
    def _():
        tail_copy(t - 3).start()
        tail_copy(t - 3).wait()

    @pl.when(t >= 3)
    def _():
        fwd_copy(t - 3).wait_send()

    @pl.when(t == images + 2)
    def _():
        near_copy(images - 1).wait_send()
        wide_copy(images - 1).wait_send()
        far_copy(images - 1).wait_send()


def mixer(x_blk, w1t, b1, w2t, b2, gain1, bias1, gain2, bias2, bc1, bc2, wc1, wc2):
    images, rows, chans = x_blk.shape
    hidden = w1t.shape[0]
    quarter = hidden // 4
    chan_hid = wc1.shape[1]
    steps = chan_hid // HID_STEP
    kept = images - TAIL
    anywhere = pl.BlockSpec(memory_space=pl.ANY)

    def const(shape):
        return pl.BlockSpec(shape, lambda t: (0,) * len(shape), pipeline_mode=pl.Buffered(1))

    dma = pltpu.SemaphoreType.DMA
    return pl.pallas_call(
        functools.partial(mixer_kernel, images),
        name="mixer",
        grid=(images + LAG,),
        in_specs=[
            pl.BlockSpec((1, rows, chans), lambda t: (jnp.minimum(t, images - 1), 0, 0)),
            pl.BlockSpec((1, rows, chans), lambda t: (jnp.clip(t - LAG, 0, kept - 1), 0, 0)),
            const((hidden, rows)),
            const((quarter, 1)),
            const((rows, hidden)),
            const((rows, 1)),
            const((1, chans)),
            const((1, chans)),
            const((1, chans)),
            const((1, chans)),
            const((steps, 1, HID_STEP)),
            const((1, chans)),
            anywhere,
            anywhere,
        ],
        out_specs=[
            pl.BlockSpec((1, rows, chans), lambda t: (jnp.clip(t - LAG, 0, kept - 1), 0, 0)),
            anywhere,
        ],
        out_shape=[
            jax.ShapeDtypeStruct((kept, rows, chans), BF16),
            jax.ShapeDtypeStruct((TAIL, 4, quarter, chans), BF16),
        ],
        scratch_shapes=[
            pltpu.VMEM((steps, chans, HID_STEP), BF16),
            pltpu.VMEM((steps, HID_STEP, chans), BF16),
            pltpu.VMEM((rows, chans), F32),
            pltpu.VMEM((rows, chans), BF16),
            pltpu.VMEM((ROW_HALF, HID_STEP), F32),
            pltpu.VMEM((ROW_HALF, HID_STEP), F32),
            pltpu.VMEM((ROW_HALF, HID_STEP), BF16),
            pltpu.VMEM((ROW_HALF, HID_STEP), BF16),
            pltpu.VMEM((2, 2, quarter, chans), F32),
            pltpu.VMEM((2, 2, quarter, chans), F32),
            pltpu.VMEM((quarter, chans), F32),
            pltpu.VMEM((quarter, chans), F32),
            pltpu.VMEM((2, quarter, chans), F32),
            pltpu.VMEM((3, 4, quarter, chans), BF16),
            dma((2, steps)),
            dma, dma((2,)),
            dma, dma((2,)),
            dma, dma((3,)),
            dma, dma((3,)),
            dma, dma((3,)),
            dma,
        ],
        compiler_params=pltpu.CompilerParams(
            vmem_limit_bytes=63 << 20, collective_id=0, has_side_effects=True, dimension_semantics=("arbitrary",)
        ),
        cost_estimate=pl.CostEstimate(
            flops=2 * images * rows * chans * 2 * (hidden + chan_hid),
            bytes_accessed=images * 6 * rows * chans,
            transcendentals=images * rows * chan_hid,
        ),
    )(x_blk, x_blk, w1t, b1, w2t, b2, gain1, bias1, gain2, bias2, bc1, bc2, wc1, wc2)


def finish_kernel(
    x_ref, g_ref, w2t_ref, b2_ref, gain_ref, bias_ref, bc1_ref, bc2_ref, wc1_hbm, wc2_hbm, done_hbm, z_hbm,
    wc1_ref, wc2_ref, acc_ref, v_ref, h_a, h_b, a_a, a_b, z_buf, move, w_sems, z_sem, in_sems, out_sems,
):
    i = pl.program_id(0)
    steps = wc1_ref.shape[0]
    kept = done_hbm.shape[0]
    lanes = move.shape[1]
    rounds = kept // lanes
    images = pl.num_programs(0)

    def read(it, k):
        return pltpu.make_async_copy(done_hbm.at[it * lanes + k], move.at[lax.rem(it, 2), k], in_sems.at[lax.rem(it, 2), k])

    def write(it, k):
        return pltpu.make_async_copy(move.at[lax.rem(it, 2), k], z_hbm.at[it * lanes + k], out_sems.at[lax.rem(it, 2), k])

    def shift(it):
        @pl.when(jnp.logical_and(it >= 1, it <= rounds))
        def _():
            for k in range(lanes):
                read(it - 1, k).wait()
                write(it - 1, k).start()

        @pl.when(jnp.logical_and(it >= 2, it <= rounds + 1))
        def _():
            for k in range(lanes):
                write(it - 2, k).wait()

        @pl.when(it < rounds)
        def _():
            for k in range(lanes):
                read(it, k).start()

    @pl.when(i == 0)
    def _():
        for j in range(steps):
            for copy in weight_copies(wc1_hbm, wc2_hbm, wc1_ref, wc2_ref, w_sems, j):
                copy.start()

    def arrive(j):
        @pl.when(i == 0)
        def _():
            for copy in weight_copies(wc1_hbm, wc2_hbm, wc1_ref, wc2_ref, w_sems, j):
                copy.wait()

        shift(i * steps + j)

    def z_copy(k):
        return pltpu.make_async_copy(z_buf.at[lax.rem(k, 2)], z_hbm.at[kept + k], z_sem.at[lax.rem(k, 2)])

    def put(cut, value):
        z_buf[lax.rem(i, 2), cut, :] = value

    g = g_ref[0].reshape(-1, g_ref.shape[3])
    channel_mix(
        x_ref, g, w2t_ref, b2_ref, gain_ref, bias_ref, bc1_ref, bc2_ref, wc1_ref, wc2_ref,
        (acc_ref, v_ref, h_a, h_b, a_a, a_b), put, arrive,
    )
    z_copy(i).start()

    @pl.when(i == images - 1)
    def _():
        shift(TAIL * steps)
        for k in range(TAIL):
            z_copy(k).wait()


def finish(x_blk, g_tail, w2t, b2, gain, bias, bc1, bc2, wc1, wc2, done):
    images, rows, chans = x_blk.shape
    hidden = w2t.shape[1]
    quarter = hidden // 4
    chan_hid = wc1.shape[1]
    steps = chan_hid // HID_STEP
    kept = images - TAIL
    anywhere = pl.BlockSpec(memory_space=pl.ANY)

    def const(shape):
        return pl.BlockSpec(shape, lambda t: (0,) * len(shape), pipeline_mode=pl.Buffered(1))

    dma = pltpu.SemaphoreType.DMA
    return pl.pallas_call(
        finish_kernel,
        name="finish",
        grid=(TAIL,),
        in_specs=[
            pl.BlockSpec((1, rows, chans), lambda i: (kept + i, 0, 0)),
            pl.BlockSpec((1, 4, quarter, chans), lambda i: (i, 0, 0, 0)),
            const((rows, hidden)),
            const((rows, 1)),
            const((1, chans)),
            const((1, chans)),
            const((steps, 1, HID_STEP)),
            const((1, chans)),
            anywhere,
            anywhere,
            anywhere,
        ],
        out_specs=anywhere,
        out_shape=jax.ShapeDtypeStruct(x_blk.shape, BF16),
        scratch_shapes=[
            pltpu.VMEM((steps, chans, HID_STEP), BF16),
            pltpu.VMEM((steps, HID_STEP, chans), BF16),
            pltpu.VMEM((rows, chans), F32),
            pltpu.VMEM((rows, chans), BF16),
            pltpu.VMEM((ROW_HALF, HID_STEP), F32),
            pltpu.VMEM((ROW_HALF, HID_STEP), F32),
            pltpu.VMEM((ROW_HALF, HID_STEP), BF16),
            pltpu.VMEM((ROW_HALF, HID_STEP), BF16),
            pltpu.VMEM((2, rows, chans), BF16),
            pltpu.VMEM((2, 2, rows, chans), BF16),
            dma((2, steps)),
            dma((2,)),
            dma((2, 2)),
            dma((2, 2)),
        ],
        compiler_params=pltpu.CompilerParams(vmem_limit_bytes=63 << 20, dimension_semantics=("arbitrary",)),
        cost_estimate=pl.CostEstimate(
            flops=2 * TAIL * rows * chans * (hidden + 2 * chan_hid),
            bytes_accessed=images * 4 * rows * chans,
            transcendentals=TAIL * rows * chan_hid,
        ),
    )(x_blk, g_tail, w2t, b2, gain, bias, bc1, bc2, wc1, wc2, done)


def solution(mesh):
    row_spec = P("dp", "sp", None)

    def local_layer(x_blk, w1_rows, b1_part, w2_cols, b2_part, w_ch1, b_ch1, w_ch2, b_ch2, ln1_gain, ln1_bias, ln2_gain, ln2_bias):
        w2t = w2_cols.T
        b2_col = b2_part[:, None]
        gain2, bias2 = ln2_gain[None, :], ln2_bias[None, :]
        bc1 = b_ch1.reshape(-1, 1, HID_STEP)
        bc2 = b_ch2[None, :]
        done, g_tail = mixer(
            x_blk, w1_rows.T, b1_part[:, None], w2t, b2_col, ln1_gain[None, :], ln1_bias[None, :], gain2, bias2, bc1, bc2, w_ch1, w_ch2
        )
        return finish(x_blk, g_tail, w2t, b2_col, gain2, bias2, bc1, bc2, w_ch1, w_ch2, done)

    in_specs = (row_spec, P("sp", None), P("sp"), P(None, "sp"), P("sp"), P(None, None), P(None), P(None, None), P(None), P(None), P(None), P(None), P(None))
    return jax.shard_map(local_layer, mesh=mesh, in_specs=in_specs, out_specs=row_spec, check_vma=False)
```

time: 1800 us -> 919 us (0.51)
  Pallas kernels: 0 us -> 911 us
  matrix products: 880 us -> 0 us
  waiting for transfers between devices: 647 us -> 0 us
  local copies, waits for them, and re-layouts: 175 us -> 7.64 us
  other arithmetic: 75.6 us -> 0 us
    pallas_call x0 -> x2, Pallas kernels: none -> 911 us  [the longest x1 847 us: mixer(): pl.pallas_call(functools.partial(mixer_kernel, images), name='mixer', gri...]
    dot_general x4 -> x0, matrix products: 880 us -> none  [the longest x1 439 us: channel_mix(): jnp.einsum('bsc,cf->bsf', normed_two, w_ch1, preferred_element_type=jnp.f...]
    reduce_scatter x1 -> x0, waiting for transfers between devices: 443 us -> none  [local_layer(): lax.psum_scatter(part_pre, 'sp', scatter_dimension=1, tiled=True)]
    all_gather x1 -> x0, waiting for transfers between devices: 204 us -> none  [local_layer(): act_full = lax.all_gather(tok_act, 'sp', axis=1, tiled=True)]
    convert_element_type x1 -> x0, local copies, waits for them, and re-layouts: 87.3 us -> none  [channel_mix(): return (mid_wide + ch_out).astype(jnp.bfloat16)]
    unnamed x23 -> x2, local copies, waits for them, and re-layouts: 87.5 us -> 4.55 us
    reduce_sum x3 -> x0, other arithmetic: 63.8 us -> none  [the longest x2 43 us: layer_norm(): var_val = jnp.mean(centred * centred, axis=-1, keepdims=True)]
  transfers between devices with their start and end apart: 2 -> 0, of which waited for: 2 -> 0; matrix products, arithmetic and copies ran while one was open for 0% -> 0% of each run, Pallas kernels for 0% -> 0%
where the time goes in v1:
time: 919 us
  Pallas kernels  911 us (99%)
    pallas_call x1, Pallas kernels, mixer(): pl.pallas_call(functools.partial(mixer_kernel, images), name='mixer', gri...  847 us
    pallas_call x1, Pallas kernels, finish(): pl.pallas_call(finish_kernel, name='finish', grid=(TAIL,), in_specs=[pl.B...  64.7 us

profile of v1, /device:TPU:0, one launch (start us, length us, event | category | flops | bytes accessed | tf_op | source)
XLA Modules:
  0.0 919.1 jit_solution(17914856973763301363)
XLA Ops:
  0.0 1.4 copy.19.b1_ref
  1.4 1.7 copy.20.b2_ref
  3.1 2.3 copy.17
  5.4 2.3 copy.18
  7.6 846.6 %mixer.1 = (bf16[30,1024,1024]{2,1,0:T(8,128)(2,1)}, bf16[2,4,128,1024]{3,2,1,0:T(8,128)(2,1)}) custom-call(bf16[32,1024,1024]{2,1,0:T(8,128)(2,1)} %x_ref.1, bf16[32,1024,1024]{2,1,0:T(8,128)(2,1)} %x_ref.1, bf16[512,1024]{1,0:T(8,128)(2,1)} %bitcast.12, f32[128,1]{1,0:T(8,128)} %copy.19.b1_ref, bf16[1024,512]{1,0:T(8,128)(2,1)} %bitcast.10, ...), custom_call_target="tpu_custom_call" | custom-call | flops 618475290624 | bytes 201326592 | tf_op jit(solution)/shard_map/mixer/pallas_call | solution.py:272
  854.2 64.7 %finish.1 = bf16[32,1024,1024]{2,1,0:T(8,128)(2,1)} custom-call(bf16[32,1024,1024]{2,1,0:T(8,128)(2,1)} %x_ref.1, bf16[2,4,128,1024]{3,2,1,0:T(8,128)(2,1)} %get-tuple-element.7.g_ref, bf16[1024,512]{1,0:T(8,128)(2,1)} %bitcast.11, f32[1024,1]{1,0:T(8,128)} %copy.20.b2_ref, f32[1,1024]{1,0:T(1,128)} %bitcast.16, f32[1,1024]{1,0:T(1,128)} %bitcast.18, ...), custom_call_target="tpu_custom_call" | custom-call | flops 36507222016 | bytes 134217728 | tf_op jit(solution)/shard_map/finish/pallas_call | solution.py:415
